TPU v7x, 256 devices: a whole 4x4x8 slice. The times are simulated.
256 devices in a mesh: exp: 32 (over x, y, core), tp: 8 (over z).
Axes of the slice: x: 4, y: 4, z: 8, core: 2. Of those that a mesh axis runs over, the one named last changes fastest.
Arguments:
- tokens: bfloat16 [896, 4096], P('exp', 'tp'), may hold values from -6 to 6
- cotangent: bfloat16 [896, 4096], P('exp', 'tp'), may hold values from -6 to 6
- experts: int32 [896, 2], P('exp'), may hold values from 0 to 7, all different within a row; in each aligned block of 28 rows (0 to 27, 28 to 55, ...) at most 8 rows name the same one
- gates: float32 [896, 2], P('exp'), may hold values from 0.1 to 0.9
- w_gate: bfloat16 [32, 4096, 2048], P('exp', None, 'tp'), may hold values from -0.09375 to 0.09375
- w_up: bfloat16 [32, 4096, 2048], P('exp', None, 'tp'), may hold values from -0.09375 to 0.09375
- w_down: bfloat16 [32, 2048, 4096], P('exp', 'tp'), may hold values from -0.0625 to 0.0625
Outputs:
- output: bfloat16 [896, 4096], P('exp', 'tp')
- input_grad: bfloat16 [896, 4096], P('exp', 'tp')
- grad_gate: bfloat16 [32, 4096, 2048], P('exp', None, 'tp')
- grad_up: bfloat16 [32, 4096, 2048], P('exp', None, 'tp')
- grad_down: bfloat16 [32, 2048, 4096], P('exp', 'tp')
Inputs may be any that keep to these rules, and one draw needn't show every extreme that they name: Each row names 2 different experts. In each aligned block of 28 rows (the rows of one index of exp) no expert is named by more than 8 rows, and in some blocks one is named by exactly 8.
All inputs are finite; a program needn't handle non-finite values.
Results may differ from a plain program's by a relative error of at most 0.017.
Values may be sent and summed in bfloat16 or wider, within the bound.
No kernel may reach another device: no remote copies, remote signals or barrier semaphores. Data moves between devices by JAX's collectives and lax.ppermute only.
A program may use at most 64 MiB of HBM per device.

v0:
```python
import functools
import math

import jax
import jax.numpy as jnp
from jax import lax
from jax.experimental import pallas as pl
from jax.experimental.pallas import tpu as pltpu
from jax.sharding import Mesh, PartitionSpec as P


EXPERTS = 8
CAP = 8

EXP_AXES = ("x", "yh", "yl", "c")
TP_AXES = ("za", "zb")
PEERS = ("zb", "x", "yh", "yl")
F32, BF16 = jnp.float32, jnp.bfloat16


def mm(a, b):
    return jnp.dot(a, b, preferred_element_type=F32)


def mm_nt(a, b):
    return lax.dot_general(a, b, (((1,), (1,)), ((), ())), preferred_element_type=F32)


def mm_tn(a, b):
    return lax.dot_general(a, b, (((0,), (0,)), ((), ())), preferred_element_type=F32)


def slot_hits(exp_ref, gate_ref, rows, group):
    n_tok = exp_ref.shape[1]
    r = lax.broadcasted_iota(jnp.int32, (rows, n_tok), 0)
    k, s = r // group, r % CAP
    first, second = exp_ref[0:1, :] == k, exp_ref[1:2, :] == k
    named = (first | second).astype(F32)
    before_of = lax.broadcasted_iota(jnp.int32, (n_tok, n_tok), 0) < lax.broadcasted_iota(
        jnp.int32, (n_tok, n_tok), 1
    )
    before = mm(named.astype(BF16), before_of.astype(F32).astype(BF16))
    hit = jnp.where(before == s.astype(F32), named, 0.0)
    gate = jnp.where(first, gate_ref[0:1, :], 0.0) + jnp.where(second, gate_ref[1:2, :], 0.0)
    return hit, hit * gate


def lane_shift(n_tok, by):
    row = lax.broadcasted_iota(jnp.int32, (n_tok, 2 * n_tok), 0)
    lane = lax.broadcasted_iota(jnp.int32, (n_tok, 2 * n_tok), 1)
    return (lane == row + by).astype(F32).astype(BF16)


def route_kernel(exp_ref, gate_ref, x_ref, g_ref, scale_ref, high_ref, low_ref, hit_ref, *, group):
    n_tok = exp_ref.shape[1]
    left, right = lane_shift(n_tok, 0), lane_shift(n_tok, n_tok)
    hit, weighted = slot_hits(exp_ref, gate_ref, EXPERTS * CAP, CAP)
    x_ref[...] = mm(hit.astype(BF16), left).astype(BF16)
    g_ref[...] = mm(hit.astype(BF16), right).astype(BF16)
    scale_ref[...] = jnp.broadcast_to(jnp.sum(weighted, axis=1, keepdims=True), scale_ref.shape)

    rows = EXPERTS * group
    hit, weighted = slot_hits(exp_ref, gate_ref, rows, group)
    high = weighted.astype(BF16)
    low = (weighted - high.astype(F32)).astype(BF16)
    same = (
        lax.broadcasted_iota(jnp.int32, (rows, rows), 0)
        == lax.broadcasted_iota(jnp.int32, (rows, rows), 1)
    )
    same = same.astype(F32).astype(BF16)
    for ref, table, side in ((high_ref, high, left), (low_ref, low, left), (hit_ref, hit, right)):
        ref[...] = mm_tn(mm(table.astype(BF16), side).astype(BF16), same).astype(BF16)


def dispatch_kernel(x_ref, g_ref, scale_ref, in_ref, out_ref):
    zb, _, yl, _, _ = out_ref.shape
    blocks, _, fblk = in_ref.shape
    for b in range(blocks):
        x = mm(x_ref[...], in_ref[b])
        g = mm(g_ref[...], in_ref[b]) * scale_ref[:, :1]
        for part, value in enumerate((x, g)):
            value = value.reshape(EXPERTS, CAP, fblk).astype(BF16)
            at = (part * blocks + b) * fblk
            for i in range(zb):
                for j in range(yl):
                    out_ref[i, :, j, :, at : at + fblk] = value


def mark_kernel(got, out_ref):
    out_ref[...] = got[0, :8, :128].astype(F32)


def rows_kernel(got, w1, w3, w2, v1, v3, v2, acts, their_acts, out_ref, up, down, total, in_sems, sems):
    pairs, _, wide = got.shape
    half, hid = wide // 2, w1.shape[1]
    steps = in_sems.shape[0]
    fblk = w1.shape[0] // steps
    loads = []
    for t in range(steps):
        span = slice(t * fblk, (t + 1) * fblk)
        block = [
            pltpu.make_async_copy(w.at[span], up.at[span, i * hid : (i + 1) * hid], in_sems.at[t, i])
            for i, w in enumerate((w1, v1, w3, v3))
        ]
        block += [
            pltpu.make_async_copy(
                w.at[:, span], down.at[i * hid : (i + 1) * hid, span], in_sems.at[t, 4 + i]
            )
            for i, w in enumerate((w2, v2))
        ]
        for load in block:
            load.start()
        loads.append(block)

    first = second = third = 0.0
    for t in range(steps):
        for load in loads[t]:
            load.wait()
        p, at = t % pairs, t // pairs * fblk
        span = slice(t * fblk, (t + 1) * fblk)
        x, g = got[p, :, at : at + fblk], got[p, :, half + at : half + at + fblk]
        first = first + mm(x, up[span, : 2 * hid])
        second = second + mm(x, up[span, 2 * hid :])
        third = third + mm_nt(g, down[:, span])
    sig = jax.nn.sigmoid(first)
    act = (first * sig * second).astype(BF16)
    d1 = (third * second * sig * (1.0 + first * (1.0 - sig))).astype(BF16)
    d3 = (third * first * sig).astype(BF16)
    for i, value in enumerate((act, d1, d3)):
        acts[i] = value[:, :hid]
        their_acts[i] = value[:, hid:]
    both = jnp.concatenate([d1, d3], axis=1)

    copies = []
    cut = fblk // 2
    for t in range(steps):
        p, at = t % pairs, t // pairs * fblk
        for i in range(2):
            span = slice(t * fblk + i * cut, t * fblk + (i + 1) * cut)
            here = at + i * cut
            total[p, :, here : here + cut] = mm(act, down[:, span]).astype(BF16)
            total[p, :, half + here : half + here + cut] = mm_nt(both, up[span, :]).astype(BF16)
        for base in (0, half):
            lanes = slice(base + at, base + at + fblk)
            copies.append(
                pltpu.make_async_copy(
                    total.at[p, :, lanes], out_ref.at[p, :, lanes], sems.at[len(copies)]
                )
            )
            copies[-1].start()
    for copy in copies:
        copy.wait()


def weight_grad_kernel(got0, got1, acts0, acts1, _, gg_ref, gu_ref, gd_ref, done_ref):
    t = pl.program_id(0)
    pairs, _, wide = got0.shape
    fblk = gg_ref.shape[0]
    p, b = lax.rem(t, pairs), lax.div(t, pairs)
    x_at = pl.ds(pl.multiple_of(b * fblk, fblk), fblk)
    g_at = pl.ds(pl.multiple_of(wide // 2 + b * fblk, fblk), fblk)
    x = jnp.concatenate([got0[p, :, x_at], got1[p, :, x_at]], axis=0)
    g = jnp.concatenate([got0[p, :, g_at], got1[p, :, g_at]], axis=0)
    act, d1, d3 = (jnp.concatenate([acts0[i], acts1[i]], axis=0) for i in range(3))
    gg_ref[...] = mm_tn(x, d1).astype(BF16)
    gu_ref[...] = mm_tn(x, d3).astype(BF16)
    gd_ref[...] = mm_tn(act, g).astype(BF16)
    done_ref[...] = jnp.zeros_like(done_ref)


def combine_kernel(high_ref, low_ref, hit_ref, home_ref, _, out_ref):
    pairs, _, wide = home_ref.shape
    blocks, _, fblk = out_ref.shape
    for b in range(blocks):
        out = 0.0
        for p in range(pairs):
            y = home_ref[p, :, b * fblk : (b + 1) * fblk]
            dx = home_ref[p, :, wide // 2 + b * fblk : wide // 2 + (b + 1) * fblk]
            out = out + mm(high_ref[...], y) + mm(low_ref[...], y) + mm(hit_ref[...], dx)
        out_ref[b] = out.astype(BF16)


VMEM = pl.BlockSpec(memory_space=pltpu.VMEM)
HBM = pl.BlockSpec(memory_space=pltpu.HBM)


def call(kernel, ins, outs, grid=(), out_specs=None, scratch=(), mib=8, flops=0, nbytes=0):
    out_specs = out_specs or [VMEM] * len(outs)
    return pl.pallas_call(
        kernel,
        grid=grid,
        in_specs=[VMEM] * ins if isinstance(ins, int) else ins,
        out_specs=out_specs,
        out_shape=[
            (pltpu.HBM if spec is HBM else jax.ShapeDtypeStruct)(shape, dtype)
            for (shape, dtype), spec in zip(outs, out_specs)
        ],
        scratch_shapes=list(scratch),
        compiler_params=pltpu.CompilerParams(vmem_limit_bytes=mib * 1024 * 1024),
        cost_estimate=pl.CostEstimate(flops=flops, bytes_accessed=nbytes, transcendentals=0),
    )


def per_device(tokens, cotangent, experts, gates, w_gate, w_up, w_down):
    za, zb, yl = (lax.axis_size(a) for a in ("za", "zb", "yl"))
    peers = math.prod(lax.axis_size(a) for a in PEERS)
    n_tok, fblk = tokens.shape
    w1, w3, w2 = w_gate[0], w_up[0], w_down[0]
    width, hid = w1.shape
    wide = za * fblk
    rows = peers // zb * CAP
    swap = [(0, 1), (1, 0)]
    v1, v3, v2 = (lax.ppermute(w, "c", swap) for w in (w1, w3, w2))

    both = jnp.concatenate([tokens, cotangent], axis=0)
    spread = jnp.broadcast_to(both[None], (za,) + both.shape)
    mine = lax.all_to_all(spread, "za", 0, 0, tiled=True)
    table = ((2 * n_tok, EXPERTS * yl * CAP), BF16)
    pick = ((EXPERTS * CAP, 2 * n_tok), BF16)
    pick_x, pick_g, scale, high, low, hit = call(
        functools.partial(route_kernel, group=yl * CAP),
        2,
        [pick, pick, ((EXPERTS * CAP, 128), F32)] + [table] * 3,
    )(experts.T, gates.T)

    (send,) = call(dispatch_kernel, 4, [((zb, EXPERTS, yl, CAP, 2 * wide), BF16)])(
        pick_x, pick_g, scale, mine
    )
    send = send.reshape(peers, CAP, 2 * wide)
    got0 = lax.all_to_all(send, PEERS, 0, 0, tiled=True).reshape(zb, rows, 2 * wide)

    (mark,) = call(mark_kernel, 1, [((8, 128), F32)])(got0)

    product = 2 * rows * width * hid
    acts, their_acts, ours = call(
        rows_kernel,
        [VMEM] + [HBM] * 6,
        [((3, rows, hid), BF16)] * 2 + [((zb, rows, 2 * wide), BF16)],
        out_specs=[VMEM, VMEM, HBM],
        scratch=[
            pltpu.VMEM((width, 4 * hid), BF16),
            pltpu.VMEM((2 * hid, width), BF16),
            pltpu.VMEM((zb, rows, 2 * wide), BF16),
            pltpu.SemaphoreType.DMA((width // fblk, 6)),
            pltpu.SemaphoreType.DMA((2 * zb * za,)),
        ],
        mib=24,
        flops=12 * product,
    )(got0, *(pltpu.with_memory_space_constraint(w, pltpu.HBM) for w in (w1, w3, w2, v1, v3, v2)))
    home = lax.all_to_all(ours.reshape(peers, CAP, 2 * wide), PEERS, 0, 0, tiled=True)
    home = home.reshape(zb, EXPERTS * yl * CAP, 2 * wide)

    got1 = lax.ppermute(got0, "c", swap)
    their_acts = lax.ppermute(their_acts, "c", swap)
    tall = pl.BlockSpec((fblk, hid), lambda t: (t, 0))
    flat = pl.BlockSpec((hid, fblk), lambda t: (0, t))
    grad_gate, grad_up, grad_down, done = call(
        weight_grad_kernel,
        5,
        [((width, hid), BF16)] * 2 + [((hid, width), BF16), ((8, 128), F32)],
        grid=(width // fblk,),
        out_specs=[tall, tall, flat, pl.BlockSpec((8, 128), lambda t: (0, 0))],
        flops=6 * product,
        nbytes=6 * width * hid,
    )(got0, got1, acts, their_acts, mark)

    (mixed,) = call(combine_kernel, 5, [((za, 2 * n_tok, fblk), BF16)])(high, low, hit, home, done)
    parts = lax.all_to_all(mixed, "za", 0, 0, tiled=True)
    total = jnp.sum(parts.astype(F32), axis=0)
    output, input_grad = total[:n_tok].astype(BF16), total[n_tok:].astype(BF16)
    return output, input_grad, grad_gate[None], grad_up[None], grad_down[None]


def solution(mesh):
    group = mesh.shape["exp"] // EXPERTS
    shape = (EXPERTS // 2, 2, group // 2, 2, mesh.shape["tp"] // 2, 2)
    fine = Mesh(mesh.devices.reshape(shape), EXP_AXES + TP_AXES)
    spec = (
        P(EXP_AXES, TP_AXES),
        P(EXP_AXES, TP_AXES),
        P(EXP_AXES, None),
        P(EXP_AXES, None),
        P(EXP_AXES, None, TP_AXES),
        P(EXP_AXES, None, TP_AXES),
        P(EXP_AXES, TP_AXES, None),
    )
    out = (spec[0], spec[1], spec[4], spec[5], spec[6])
    return jax.shard_map(per_device, mesh=fine, in_specs=spec, out_specs=out, check_vma=False)
```

profile of v0, /device:TPU:2, one launch (start us, length us, event | category | flops | bytes accessed | tf_op | source)
XLA Modules:
  0.0 114.1 jit_solution(4424867999378601484)
XLA Ops:
  0.6 0.8 pad_maximum_fusion
  1.4 0.7 broadcast_in_dim.15
  2.1 8.5 %all-to-all-start = ((bf16[4,56,512]{2,1,0:T(8,128)(2,1)}), bf16[4,56,512]{2,1,0:T(8,128)(2,1)S(1)}, u32[]{:S(2)}, u32[]{:S(2)}) async-start(bf16[4,56,512]{2,1,0:T(8,128)(2,1)} %broadcast_in_dim.15), calls=%async_computation | async-start | bytes 458752 | tf_op jit(solution)/shard_map/all_to_all | solution.py:217
  10.6 0.0 copy-start.1
  10.6 0.7 copy-done.1
  11.3 0.0 copy-start.2
  11.3 0.7 copy-done.2
  11.9 0.6 shard_map.110
  12.5 8.2 %all-to-all-done.in_ref = bf16[4,56,512]{2,1,0:T(8,128)(2,1)S(1)} async-done(((bf16[4,56,512]{2,1,0:T(8,128)(2,1)}), bf16[4,56,512]{2,1,0:T(8,128)(2,1)S(1)}, u32[]{:S(2)}, u32[]{:S(2)}) %all-to-all-start) | async-done | bytes 229408 | tf_op jit(solution)/shard_map/all_to_all | solution.py:217
  20.7 0.3 shard_map.111
  21.0 0.0 copy-start
  21.0 1.3 %copy-done = bf16[2,8,2,8,4096]{4,3,2,1,0:T(8,128)(2,1)} copy-done((bf16[2,8,2,8,4096]{4,3,2,1,0:T(8,128)(2,1)}, bf16[2,8,2,8,4096]{4,3,2,1,0:T(8,128)(2,1)S(1)}, u32[]{:S(2)}) %copy-start) | copy-done | bytes 2097176
  22.3 8.0 %all-to-all-start.1 = ((bf16[32,8,4096]{2,1,0:T(8,128)(2,1)}), bf16[32,8,4096]{2,1,0:T(8,128)(2,1)S(1)}, u32[]{:S(2)}, u32[]{:S(2)}) async-start(bf16[32,8,4096]{2,1,0:T(8,128)(2,1)} %bitcast.16), calls=%async_computation.1 | async-start | bytes 4194304 | tf_op jit(solution)/shard_map/all_to_all | solution.py:230
  30.4 0.1 collective-permute-start
  30.5 0.5 collective-permute-start.1
  31.0 0.1 collective-permute-start.2
  31.1 3.8 %collective-permute-done.v1 = bf16[4096,256]{1,0:T(8,128)(2,1)S(1)} collective-permute-done((bf16[4096,256]{1,0:T(8,128)(2,1)}, bf16[4096,256]{1,0:T(8,128)(2,1)S(1)}, u32[]{:S(2)}, u32[]{:S(2)}) %collective-permute-start) | collective-permute-done | bytes 2097184 | tf_op jit(solution)/shard_map/ppermute | solution.py:213
  34.8 0.0 copy-start.3
  34.8 3.0 %collective-permute-done.1.v3 = bf16[4096,256]{1,0:T(8,128)(2,1)S(1)} collective-permute-done((bf16[4096,256]{1,0:T(8,128)(2,1)}, bf16[4096,256]{1,0:T(8,128)(2,1)S(1)}, u32[]{:S(2)}, u32[]{:S(2)}) %collective-permute-start.1) | collective-permute-done | bytes 2097184 | tf_op jit(solution)/shard_map/ppermute | solution.py:213
  37.8 0.0 copy-done.3
  37.8 0.0 copy-start.4
  37.8 1.3 %copy-done.4 = bf16[4096,256]{1,0:T(8,128)(2,1)} copy-done((bf16[4096,256]{1,0:T(8,128)(2,1)}, bf16[4096,256]{1,0:T(8,128)(2,1)S(1)}, u32[]{:S(2)}) %copy-start.4) | copy-done | bytes 2097176
  39.1 1.8 %collective-permute-done.2.v2 = bf16[256,4096]{1,0:T(8,128)(2,1)} collective-permute-done((bf16[256,4096]{1,0:T(8,128)(2,1)}, bf16[256,4096]{1,0:T(8,128)(2,1)}, u32[]{:S(2)}, u32[]{:S(2)}) %collective-permute-start.2) | collective-permute-done | bytes 2097184 | tf_op jit(solution)/shard_map/ppermute | solution.py:213
  40.9 14.6 %all-to-all-done.1 = bf16[32,8,4096]{2,1,0:T(8,128)(2,1)S(1)} async-done(((bf16[32,8,4096]{2,1,0:T(8,128)(2,1)}), bf16[32,8,4096]{2,1,0:T(8,128)(2,1)S(1)}, u32[]{:S(2)}, u32[]{:S(2)}) %all-to-all-start.1) | async-done | bytes 2097184 | tf_op jit(solution)/shard_map/all_to_all | solution.py:230
  55.5 9.4 %shard_map.112 = (bf16[3,128,256]{2,1,0:T(8,128)(2,1)S(1)}, bf16[3,128,256]{2,1,0:T(8,128)(2,1)S(1)}, bf16[2,128,4096]{2,1,0:T(8,128)(2,1)}) custom-call(bf16[2,128,4096]{2,1,0:T(8,128)(2,1)S(1)} %bitcast.12, bf16[4096,256]{1,0:T(8,128)(2,1)} %bitcast.20, bf16[4096,256]{1,0:T(8,128)(2,1)} %bitcast.22, bf16[256,4096]{1,0:T(8,128)(2,1)} %bitcast.24, ...), custom_call_target="tpu_custom_call" | custom-call | flops 3221225472 | tf_op jit(solution)/shard_map/pallas_call | solution.py:235
  64.9 6.2 %all-to-all-start.2 = ((bf16[32,8,4096]{2,1,0:T(8,128)(2,1)}), bf16[32,8,4096]{2,1,0:T(8,128)(2,1)}, u32[]{:S(2)}, u32[]{:S(2)}) async-start(bf16[32,8,4096]{2,1,0:T(8,128)(2,1)} %bitcast.25), calls=%async_computation.2 | async-start | bytes 4194304 | tf_op jit(solution)/shard_map/all_to_all | solution.py:250
  71.2 0.1 collective-permute-start.3
  71.3 0.5 collective-permute-start.4
  71.8 3.9 %collective-permute-done.4.acts1 = bf16[3,128,256]{2,1,0:T(8,128)(2,1)S(1)} collective-permute-done((bf16[3,128,256]{2,1,0:T(8,128)(2,1)S(1)}, bf16[3,128,256]{2,1,0:T(8,128)(2,1)S(1)}, u32[]{:S(2)}, u32[]{:S(2)}) %collective-permute-start.4) | collective-permute-done | bytes 196640 | tf_op jit(solution)/shard_map/ppermute | solution.py:254
  75.7 0.0 collective-permute-done.3.got1
  75.7 5.3 %shard_map.114 = (bf16[4096,256]{1,0:T(8,128)(2,1)}, bf16[4096,256]{1,0:T(8,128)(2,1)}, bf16[256,4096]{1,0:T(8,128)(2,1)}, f32[8,128]{1,0:T(8,128)S(1)}) custom-call(bf16[2,128,4096]{2,1,0:T(8,128)(2,1)S(1)} %bitcast.15, bf16[2,128,4096]{2,1,0:T(8,128)(2,1)S(1)} %collective-permute-done.3.got1, bf16[3,128,256]{2,1,0:T(8,128)(2,1)S(1)} %get-tuple-element.25.acts0, ...), custom_call_target="tpu_custom_call" | custom-call | flops 1610612736 | bytes 6291456 | tf_op jit(solution)/shard_map/pallas_call | solution.py:257
  81.0 15.6 %all-to-all-done.2 = bf16[32,8,4096]{2,1,0:T(8,128)(2,1)} async-done(((bf16[32,8,4096]{2,1,0:T(8,128)(2,1)}), bf16[32,8,4096]{2,1,0:T(8,128)(2,1)}, u32[]{:S(2)}, u32[]{:S(2)}) %all-to-all-start.2) | async-done | bytes 2097184 | tf_op jit(solution)/shard_map/all_to_all | solution.py:250
  96.6 2.2 %shard_map.115 = bf16[4,56,512]{2,1,0:T(8,128)(2,1)S(1)} custom-call(bf16[56,128]{1,0:T(8,128)(2,1)S(1)} %get-tuple-element.18.high_ref, bf16[56,128]{1,0:T(8,128)(2,1)S(1)} %get-tuple-element.19.low_ref, bf16[56,128]{1,0:T(8,128)(2,1)S(1)} %get-tuple-element.20.hit_ref, bf16[2,128,4096]{2,1,0:T(8,128)(2,1)} %bitcast.8.home_ref, ...), custom_call_target="tpu_custom_call" | custom-call | tf_op jit(solution)/shard_map/pallas_call | solution.py:267
  98.7 14.7 %all_to_all.20 = bf16[4,56,512]{2,1,0:T(8,128)(2,1)S(1)} all-to-all(bf16[4,56,512]{2,1,0:T(8,128)(2,1)S(1)} %shard_map.115), channel_id=1, replica_groups=mesh['x'=4,'yh'=2,'yl'=2,'c'=2,'za'=4,'zb'=2] {'za'}, dimensions={0} | all-to-all | bytes 458752 | tf_op jit(solution)/shard_map/all_to_all | solution.py:268
  113.4 0.6 fusion
  (2 shorter events, 0.0 us)
Async XLA Ops:
  2.1 18.6 %all-to-all-start = ((bf16[4,56,512]{2,1,0:T(8,128)(2,1)}), bf16[4,56,512]{2,1,0:T(8,128)(2,1)S(1)}, u32[]{:S(2)}, u32[]{:S(2)}) async-start(bf16[4,56,512]{2,1,0:T(8,128)(2,1)} %broadcast_in_dim.15), calls=%async_computation | async-start | bytes 458752 | tf_op jit(solution)/shard_map/all_to_all | solution.py:217
  10.6 0.7 copy-start.1
  11.3 0.7 copy-start.2
  21.0 1.3 %copy-start = (bf16[2,8,2,8,4096]{4,3,2,1,0:T(8,128)(2,1)}, bf16[2,8,2,8,4096]{4,3,2,1,0:T(8,128)(2,1)S(1)}, u32[]{:S(2)}) copy-start(bf16[2,8,2,8,4096]{4,3,2,1,0:T(8,128)(2,1)S(1)} %shard_map.111) | copy-start | bytes 6291460
  22.3 33.2 %all-to-all-start.1 = ((bf16[32,8,4096]{2,1,0:T(8,128)(2,1)}), bf16[32,8,4096]{2,1,0:T(8,128)(2,1)S(1)}, u32[]{:S(2)}, u32[]{:S(2)}) async-start(bf16[32,8,4096]{2,1,0:T(8,128)(2,1)} %bitcast.16), calls=%async_computation.1 | async-start | bytes 4194304 | tf_op jit(solution)/shard_map/all_to_all | solution.py:230
  30.4 4.5 %collective-permute-start = (bf16[4096,256]{1,0:T(8,128)(2,1)}, bf16[4096,256]{1,0:T(8,128)(2,1)S(1)}, u32[]{:S(2)}, u32[]{:S(2)}) collective-permute-start(bf16[4096,256]{1,0:T(8,128)(2,1)} %bitcast.19), channel_id=1, source_target_pairs={{0,8},{8,0},{1,9},{9,1},{2,10},{10,2},{3,11},{11,3},{4,12},{12,4},... | collective-permute-start | bytes 6291464 | tf_op jit(solution)/shard_map/ppermute | solution.py:213
  30.5 7.4 %collective-permute-start.1 = (bf16[4096,256]{1,0:T(8,128)(2,1)}, bf16[4096,256]{1,0:T(8,128)(2,1)S(1)}, u32[]{:S(2)}, u32[]{:S(2)}) collective-permute-start(bf16[4096,256]{1,0:T(8,128)(2,1)} %bitcast.21), channel_id=1, source_target_pairs={{0,8},{8,0},{1,9},{9,1},{2,10},{10,2},{3,11},{11,3},{4,12},{12,4},... | collective-permute-start | bytes 6291464 | tf_op jit(solution)/shard_map/ppermute | solution.py:213
  31.0 10.0 %collective-permute-start.2 = (bf16[256,4096]{1,0:T(8,128)(2,1)}, bf16[256,4096]{1,0:T(8,128)(2,1)}, u32[]{:S(2)}, u32[]{:S(2)}) collective-permute-start(bf16[256,4096]{1,0:T(8,128)(2,1)} %bitcast.23), channel_id=1, source_target_pairs={{0,8},{8,0},{1,9},{9,1},{2,10},{10,2},{3,11},{11,3},{4,12},{12,4},... | collective-permute-start | bytes 6291464 | tf_op jit(solution)/shard_map/ppermute | solution.py:213
  34.8 3.0 %copy-start.3 = (bf16[4096,256]{1,0:T(8,128)(2,1)}, bf16[4096,256]{1,0:T(8,128)(2,1)S(1)}, u32[]{:S(2)}) copy-start(bf16[4096,256]{1,0:T(8,128)(2,1)S(1)} %collective-permute-done.v1) | copy-start | bytes 6291460
  37.8 1.3 %copy-start.4 = (bf16[4096,256]{1,0:T(8,128)(2,1)}, bf16[4096,256]{1,0:T(8,128)(2,1)S(1)}, u32[]{:S(2)}) copy-start(bf16[4096,256]{1,0:T(8,128)(2,1)S(1)} %collective-permute-done.1.v3) | copy-start | bytes 6291460
  64.9 31.6 %all-to-all-start.2 = ((bf16[32,8,4096]{2,1,0:T(8,128)(2,1)}), bf16[32,8,4096]{2,1,0:T(8,128)(2,1)}, u32[]{:S(2)}, u32[]{:S(2)}) async-start(bf16[32,8,4096]{2,1,0:T(8,128)(2,1)} %bitcast.25), calls=%async_computation.2 | async-start | bytes 4194304 | tf_op jit(solution)/shard_map/all_to_all | solution.py:250
  71.2 4.5 %collective-permute-start.3 = (bf16[2,128,4096]{2,1,0:T(8,128)(2,1)S(1)}, bf16[2,128,4096]{2,1,0:T(8,128)(2,1)S(1)}, u32[]{:S(2)}, u32[]{:S(2)}) collective-permute-start(bf16[2,128,4096]{2,1,0:T(8,128)(2,1)S(1)} %bitcast.13), channel_id=1, source_target_pairs={{0,8},{8,0},{1,9},{9,1},{2,10},{10,2},{3,11},{11,3},{4,12},{12,4},... | collective-permute-start | bytes 6291464 | tf_op jit(solution)/shard_map/ppermute | solution.py:253
  71.3 4.4 %collective-permute-start.4 = (bf16[3,128,256]{2,1,0:T(8,128)(2,1)S(1)}, bf16[3,128,256]{2,1,0:T(8,128)(2,1)S(1)}, u32[]{:S(2)}, u32[]{:S(2)}) collective-permute-start(bf16[3,128,256]{2,1,0:T(8,128)(2,1)S(1)} %get-tuple-element.26), channel_id=1, source_target_pairs={{0,8},{8,0},{1,9},{9,1},{2,10},{10,2},{3,11},{11,3},{4,12},{12,4},... | collective-permute-start | bytes 589832 | tf_op jit(solution)/shard_map/ppermute | solution.py:254
where the time goes:
time: 115 us; the launch traced here: 114 us
  waiting for transfers between devices  50.8 us (44%)
  starting transfers between devices  24 us (21%)
  Pallas kernels  17.7 us (15%)
  blocking collectives  14.7 us (13%)
  local copies, waits for them, and re-layouts  5.33 us (5%)
    all_to_all x1, waiting for transfers between devices, per_device(): lax.all_to_all(ours.reshape(peers, CAP, 2 * wide), PEERS, 0, 0, tiled=True)  15.6 us
    all_to_all x1, blocking collectives, per_device(): parts = lax.all_to_all(mixed, 'za', 0, 0, tiled=True)  14.7 us
    all_to_all x1, waiting for transfers between devices, per_device(): lax.all_to_all(send, PEERS, 0, 0, tiled=True).reshape(zb, rows, 2 * wide)  14.6 us
    pallas_call x1, Pallas kernels, per_device(): call(rows_kernel, [VMEM] + [HBM] * 6, [((3, rows, hid), BF16)] * 2 + [((z...  9.42 us
    ppermute x3, waiting for transfers between devices, per_device(): v1, v3, v2 = (lax.ppermute(w, 'c', swap) for w in (w1, w3, w2))  8.56 us
    all_to_all x1, starting transfers between devices, per_device(): mine = lax.all_to_all(spread, 'za', 0, 0, tiled=True)  8.46 us
    all_to_all x1, waiting for transfers between devices, per_device(): mine = lax.all_to_all(spread, 'za', 0, 0, tiled=True)  8.17 us
    all_to_all x1, starting transfers between devices, per_device(): lax.all_to_all(send, PEERS, 0, 0, tiled=True).reshape(zb, rows, 2 * wide)  8.02 us
  transfers between devices with their start and end apart: 8, of which 7 were waited for; matrix products, arithmetic and copies ran while one was open for 0% of the time, Pallas kernels for 5%

commit v1 on v0

--- a/solution.py
+++ b/solution.py
@@ -168,16 +168,12 @@
     done_ref[...] = jnp.zeros_like(done_ref)
 
 
-def combine_kernel(high_ref, low_ref, hit_ref, home_ref, _, out_ref):
-    pairs, _, wide = home_ref.shape
-    blocks, _, fblk = out_ref.shape
-    for b in range(blocks):
-        out = 0.0
-        for p in range(pairs):
-            y = home_ref[p, :, b * fblk : (b + 1) * fblk]
-            dx = home_ref[p, :, wide // 2 + b * fblk : wide // 2 + (b + 1) * fblk]
-            out = out + mm(high_ref[...], y) + mm(low_ref[...], y) + mm(hit_ref[...], dx)
-        out_ref[b] = out.astype(BF16)
+def combine_kernel(high_ref, low_ref, hit_ref, y_ref, dx_ref, _, out_ref):
+    out = 0.0
+    for p in range(y_ref.shape[0]):
+        out = out + mm(high_ref[...], y_ref[p]) + mm(low_ref[...], y_ref[p])
+        out = out + mm(hit_ref[...], dx_ref[p])
+    out_ref[0] = out.astype(BF16)
 
 
 VMEM = pl.BlockSpec(memory_space=pltpu.VMEM)
@@ -264,7 +260,16 @@
         nbytes=6 * width * hid,
     )(got0, got1, acts, their_acts, mark)
 
-    (mixed,) = call(combine_kernel, 5, [((za, 2 * n_tok, fblk), BF16)])(high, low, hit, home, done)
+    home = pltpu.with_memory_space_constraint(home, pltpu.HBM)
+    block = (zb, EXPERTS * yl * CAP, fblk)
+    (mixed,) = call(
+        combine_kernel,
+        [VMEM] * 3
+        + [pl.BlockSpec(block, lambda b: (0, 0, b)), pl.BlockSpec(block, lambda b: (0, 0, za + b)), VMEM],
+        [((za, 2 * n_tok, fblk), BF16)],
+        grid=(za,),
+        out_specs=[pl.BlockSpec((1, 2 * n_tok, fblk), lambda b: (b, 0, 0))],
+    )(high, low, hit, home, home, done)
     parts = lax.all_to_all(mixed, "za", 0, 0, tiled=True)
     total = jnp.sum(parts.astype(F32), axis=0)
     output, input_grad = total[:n_tok].astype(BF16), total[n_tok:].astype(BF16)

time: 115 us -> 115 us (level)
  no operation moved by 1% of the time
where the time goes in v1:
time: 115 us
  waiting for transfers between devices  50.8 us (44%)
  starting transfers between devices  24 us (21%)
  Pallas kernels  18.5 us (16%)
  blocking collectives  14.7 us (13%)
  local copies, waits for them, and re-layouts  5.33 us (5%)
    all_to_all x1, waiting for transfers between devices, per_device(): lax.all_to_all(ours.reshape(peers, CAP, 2 * wide), PEERS, 0, 0, tiled=True)  15.6 us
    all_to_all x1, blocking collectives, per_device(): parts = lax.all_to_all(mixed, 'za', 0, 0, tiled=True)  14.7 us
    all_to_all x1, waiting for transfers between devices, per_device(): lax.all_to_all(send, PEERS, 0, 0, tiled=True).reshape(zb, rows, 2 * wide)  14.6 us
    pallas_call x1, Pallas kernels, per_device(): call(rows_kernel, [VMEM] + [HBM] * 6, [((3, rows, hid), BF16)] * 2 + [((z...  9.42 us
    ppermute x3, waiting for transfers between devices, per_device(): v1, v3, v2 = (lax.ppermute(w, 'c', swap) for w in (w1, w3, w2))  8.56 us
    all_to_all x1, starting transfers between devices, per_device(): mine = lax.all_to_all(spread, 'za', 0, 0, tiled=True)  8.46 us
    all_to_all x1, waiting for transfers between devices, per_device(): mine = lax.all_to_all(spread, 'za', 0, 0, tiled=True)  8.17 us
    all_to_all x1, starting transfers between devices, per_device(): lax.all_to_all(send, PEERS, 0, 0, tiled=True).reshape(zb, rows, 2 * wide)  8.02 us
  transfers between devices with their start and end apart: 8, of which 7 were waited for; matrix products, arithmetic and copies ran while one was open for 0% of the time, Pallas kernels for 5%

profile of v1, /device:TPU:2, one launch (start us, length us, event | category | flops | bytes accessed | tf_op | source)
XLA Modules:
  0.0 114.8 jit_solution(6637616354947440486)
XLA Ops:
  0.6 0.8 pad_maximum_fusion
  1.4 0.7 broadcast_in_dim.15
  2.1 8.5 %all-to-all-start = ((bf16[4,56,512]{2,1,0:T(8,128)(2,1)}), bf16[4,56,512]{2,1,0:T(8,128)(2,1)S(1)}, u32[]{:S(2)}, u32[]{:S(2)}) async-start(bf16[4,56,512]{2,1,0:T(8,128)(2,1)} %broadcast_in_dim.15), calls=%async_computation | async-start | bytes 458752 | tf_op jit(solution)/shard_map/all_to_all | solution.py:213
  10.6 0.0 copy-start.1
  10.6 0.7 copy-done.1
  11.3 0.0 copy-start.2
  11.3 0.7 copy-done.2
  11.9 0.6 shard_map.110
  12.5 8.2 %all-to-all-done.in_ref = bf16[4,56,512]{2,1,0:T(8,128)(2,1)S(1)} async-done(((bf16[4,56,512]{2,1,0:T(8,128)(2,1)}), bf16[4,56,512]{2,1,0:T(8,128)(2,1)S(1)}, u32[]{:S(2)}, u32[]{:S(2)}) %all-to-all-start) | async-done | bytes 229408 | tf_op jit(solution)/shard_map/all_to_all | solution.py:213
  20.7 0.3 shard_map.111
  21.0 0.0 copy-start
  21.0 1.3 %copy-done = bf16[2,8,2,8,4096]{4,3,2,1,0:T(8,128)(2,1)} copy-done((bf16[2,8,2,8,4096]{4,3,2,1,0:T(8,128)(2,1)}, bf16[2,8,2,8,4096]{4,3,2,1,0:T(8,128)(2,1)S(1)}, u32[]{:S(2)}) %copy-start) | copy-done | bytes 2097176
  22.3 8.0 %all-to-all-start.1 = ((bf16[32,8,4096]{2,1,0:T(8,128)(2,1)}), bf16[32,8,4096]{2,1,0:T(8,128)(2,1)S(1)}, u32[]{:S(2)}, u32[]{:S(2)}) async-start(bf16[32,8,4096]{2,1,0:T(8,128)(2,1)} %bitcast.16), calls=%async_computation.1 | async-start | bytes 4194304 | tf_op jit(solution)/shard_map/all_to_all | solution.py:226
  30.4 0.1 collective-permute-start
  30.5 0.5 collective-permute-start.1
  31.0 0.1 collective-permute-start.2
  31.1 3.8 %collective-permute-done.v1 = bf16[4096,256]{1,0:T(8,128)(2,1)S(1)} collective-permute-done((bf16[4096,256]{1,0:T(8,128)(2,1)}, bf16[4096,256]{1,0:T(8,128)(2,1)S(1)}, u32[]{:S(2)}, u32[]{:S(2)}) %collective-permute-start) | collective-permute-done | bytes 2097184 | tf_op jit(solution)/shard_map/ppermute | solution.py:209
  34.8 0.0 copy-start.3
  34.8 3.0 %collective-permute-done.1.v3 = bf16[4096,256]{1,0:T(8,128)(2,1)S(1)} collective-permute-done((bf16[4096,256]{1,0:T(8,128)(2,1)}, bf16[4096,256]{1,0:T(8,128)(2,1)S(1)}, u32[]{:S(2)}, u32[]{:S(2)}) %collective-permute-start.1) | collective-permute-done | bytes 2097184 | tf_op jit(solution)/shard_map/ppermute | solution.py:209
  37.8 0.0 copy-done.3
  37.8 0.0 copy-start.4
  37.8 1.3 %copy-done.4 = bf16[4096,256]{1,0:T(8,128)(2,1)} copy-done((bf16[4096,256]{1,0:T(8,128)(2,1)}, bf16[4096,256]{1,0:T(8,128)(2,1)S(1)}, u32[]{:S(2)}) %copy-start.4) | copy-done | bytes 2097176
  39.1 1.8 %collective-permute-done.2.v2 = bf16[256,4096]{1,0:T(8,128)(2,1)} collective-permute-done((bf16[256,4096]{1,0:T(8,128)(2,1)}, bf16[256,4096]{1,0:T(8,128)(2,1)}, u32[]{:S(2)}, u32[]{:S(2)}) %collective-permute-start.2) | collective-permute-done | bytes 2097184 | tf_op jit(solution)/shard_map/ppermute | solution.py:209
  40.9 14.6 %all-to-all-done.1 = bf16[32,8,4096]{2,1,0:T(8,128)(2,1)S(1)} async-done(((bf16[32,8,4096]{2,1,0:T(8,128)(2,1)}), bf16[32,8,4096]{2,1,0:T(8,128)(2,1)S(1)}, u32[]{:S(2)}, u32[]{:S(2)}) %all-to-all-start.1) | async-done | bytes 2097184 | tf_op jit(solution)/shard_map/all_to_all | solution.py:226
  55.5 9.4 %shard_map.112 = (bf16[3,128,256]{2,1,0:T(8,128)(2,1)S(1)}, bf16[3,128,256]{2,1,0:T(8,128)(2,1)S(1)}, bf16[2,128,4096]{2,1,0:T(8,128)(2,1)}) custom-call(bf16[2,128,4096]{2,1,0:T(8,128)(2,1)S(1)} %bitcast.12, bf16[4096,256]{1,0:T(8,128)(2,1)} %bitcast.20, bf16[4096,256]{1,0:T(8,128)(2,1)} %bitcast.22, bf16[256,4096]{1,0:T(8,128)(2,1)} %bitcast.24, ...), custom_call_target="tpu_custom_call" | custom-call | flops 3221225472 | tf_op jit(solution)/shard_map/pallas_call | solution.py:231
  64.9 6.2 %all-to-all-start.2 = ((bf16[32,8,4096]{2,1,0:T(8,128)(2,1)}), bf16[32,8,4096]{2,1,0:T(8,128)(2,1)}, u32[]{:S(2)}, u32[]{:S(2)}) async-start(bf16[32,8,4096]{2,1,0:T(8,128)(2,1)} %bitcast.25), calls=%async_computation.2 | async-start | bytes 4194304 | tf_op jit(solution)/shard_map/all_to_all | solution.py:246
  71.2 0.1 collective-permute-start.3
  71.3 0.5 collective-permute-start.4
  71.8 3.9 %collective-permute-done.4.acts1 = bf16[3,128,256]{2,1,0:T(8,128)(2,1)S(1)} collective-permute-done((bf16[3,128,256]{2,1,0:T(8,128)(2,1)S(1)}, bf16[3,128,256]{2,1,0:T(8,128)(2,1)S(1)}, u32[]{:S(2)}, u32[]{:S(2)}) %collective-permute-start.4) | collective-permute-done | bytes 196640 | tf_op jit(solution)/shard_map/ppermute | solution.py:250
  75.7 0.0 collective-permute-done.3.got1
  75.7 5.3 %shard_map.114 = (bf16[4096,256]{1,0:T(8,128)(2,1)}, bf16[4096,256]{1,0:T(8,128)(2,1)}, bf16[256,4096]{1,0:T(8,128)(2,1)}, f32[8,128]{1,0:T(8,128)S(1)}) custom-call(bf16[2,128,4096]{2,1,0:T(8,128)(2,1)S(1)} %bitcast.15, bf16[2,128,4096]{2,1,0:T(8,128)(2,1)S(1)} %collective-permute-done.3.got1, bf16[3,128,256]{2,1,0:T(8,128)(2,1)S(1)} %get-tuple-element.25.acts0, ...), custom_call_target="tpu_custom_call" | custom-call | flops 1610612736 | bytes 6291456 | tf_op jit(solution)/shard_map/pallas_call | solution.py:253
  81.0 15.6 %all-to-all-done.2 = bf16[32,8,4096]{2,1,0:T(8,128)(2,1)} async-done(((bf16[32,8,4096]{2,1,0:T(8,128)(2,1)}), bf16[32,8,4096]{2,1,0:T(8,128)(2,1)}, u32[]{:S(2)}, u32[]{:S(2)}) %all-to-all-start.2) | async-done | bytes 2097184 | tf_op jit(solution)/shard_map/all_to_all | solution.py:246
  96.6 2.9 %shard_map.115 = bf16[4,56,512]{2,1,0:T(8,128)(2,1)S(1)} custom-call(bf16[56,128]{1,0:T(8,128)(2,1)S(1)} %get-tuple-element.18.high_ref, bf16[56,128]{1,0:T(8,128)(2,1)S(1)} %get-tuple-element.19.low_ref, bf16[56,128]{1,0:T(8,128)(2,1)S(1)} %get-tuple-element.20.hit_ref, bf16[2,128,4096]{2,1,0:T(8,128)(2,1)} %bitcast.8.y_ref.dx_ref, ...), custom_call_target="tpu_custom_call" | custom-call | tf_op jit(solution)/shard_map/pallas_call | solution.py:265
  99.5 14.7 %all_to_all.20 = bf16[4,56,512]{2,1,0:T(8,128)(2,1)S(1)} all-to-all(bf16[4,56,512]{2,1,0:T(8,128)(2,1)S(1)} %shard_map.115), channel_id=1, replica_groups=mesh['x'=4,'yh'=2,'yl'=2,'c'=2,'za'=4,'zb'=2] {'za'}, dimensions={0} | all-to-all | bytes 458752 | tf_op jit(solution)/shard_map/all_to_all | solution.py:273
  114.2 0.6 fusion
  (2 shorter events, 0.0 us)
Async XLA Ops:
  2.1 18.6 %all-to-all-start = ((bf16[4,56,512]{2,1,0:T(8,128)(2,1)}), bf16[4,56,512]{2,1,0:T(8,128)(2,1)S(1)}, u32[]{:S(2)}, u32[]{:S(2)}) async-start(bf16[4,56,512]{2,1,0:T(8,128)(2,1)} %broadcast_in_dim.15), calls=%async_computation | async-start | bytes 458752 | tf_op jit(solution)/shard_map/all_to_all | solution.py:213
  10.6 0.7 copy-start.1
  11.3 0.7 copy-start.2
  21.0 1.3 %copy-start = (bf16[2,8,2,8,4096]{4,3,2,1,0:T(8,128)(2,1)}, bf16[2,8,2,8,4096]{4,3,2,1,0:T(8,128)(2,1)S(1)}, u32[]{:S(2)}) copy-start(bf16[2,8,2,8,4096]{4,3,2,1,0:T(8,128)(2,1)S(1)} %shard_map.111) | copy-start | bytes 6291460
  22.3 33.2 %all-to-all-start.1 = ((bf16[32,8,4096]{2,1,0:T(8,128)(2,1)}), bf16[32,8,4096]{2,1,0:T(8,128)(2,1)S(1)}, u32[]{:S(2)}, u32[]{:S(2)}) async-start(bf16[32,8,4096]{2,1,0:T(8,128)(2,1)} %bitcast.16), calls=%async_computation.1 | async-start | bytes 4194304 | tf_op jit(solution)/shard_map/all_to_all | solution.py:226
  30.4 4.5 %collective-permute-start = (bf16[4096,256]{1,0:T(8,128)(2,1)}, bf16[4096,256]{1,0:T(8,128)(2,1)S(1)}, u32[]{:S(2)}, u32[]{:S(2)}) collective-permute-start(bf16[4096,256]{1,0:T(8,128)(2,1)} %bitcast.19), channel_id=1, source_target_pairs={{0,8},{8,0},{1,9},{9,1},{2,10},{10,2},{3,11},{11,3},{4,12},{12,4},... | collective-permute-start | bytes 6291464 | tf_op jit(solution)/shard_map/ppermute | solution.py:209
  30.5 7.4 %collective-permute-start.1 = (bf16[4096,256]{1,0:T(8,128)(2,1)}, bf16[4096,256]{1,0:T(8,128)(2,1)S(1)}, u32[]{:S(2)}, u32[]{:S(2)}) collective-permute-start(bf16[4096,256]{1,0:T(8,128)(2,1)} %bitcast.21), channel_id=1, source_target_pairs={{0,8},{8,0},{1,9},{9,1},{2,10},{10,2},{3,11},{11,3},{4,12},{12,4},... | collective-permute-start | bytes 6291464 | tf_op jit(solution)/shard_map/ppermute | solution.py:209
  31.0 10.0 %collective-permute-start.2 = (bf16[256,4096]{1,0:T(8,128)(2,1)}, bf16[256,4096]{1,0:T(8,128)(2,1)}, u32[]{:S(2)}, u32[]{:S(2)}) collective-permute-start(bf16[256,4096]{1,0:T(8,128)(2,1)} %bitcast.23), channel_id=1, source_target_pairs={{0,8},{8,0},{1,9},{9,1},{2,10},{10,2},{3,11},{11,3},{4,12},{12,4},... | collective-permute-start | bytes 6291464 | tf_op jit(solution)/shard_map/ppermute | solution.py:209
  34.8 3.0 %copy-start.3 = (bf16[4096,256]{1,0:T(8,128)(2,1)}, bf16[4096,256]{1,0:T(8,128)(2,1)S(1)}, u32[]{:S(2)}) copy-start(bf16[4096,256]{1,0:T(8,128)(2,1)S(1)} %collective-permute-done.v1) | copy-start | bytes 6291460
  37.8 1.3 %copy-start.4 = (bf16[4096,256]{1,0:T(8,128)(2,1)}, bf16[4096,256]{1,0:T(8,128)(2,1)S(1)}, u32[]{:S(2)}) copy-start(bf16[4096,256]{1,0:T(8,128)(2,1)S(1)} %collective-permute-done.1.v3) | copy-start | bytes 6291460
  64.9 31.6 %all-to-all-start.2 = ((bf16[32,8,4096]{2,1,0:T(8,128)(2,1)}), bf16[32,8,4096]{2,1,0:T(8,128)(2,1)}, u32[]{:S(2)}, u32[]{:S(2)}) async-start(bf16[32,8,4096]{2,1,0:T(8,128)(2,1)} %bitcast.25), calls=%async_computation.2 | async-start | bytes 4194304 | tf_op jit(solution)/shard_map/all_to_all | solution.py:246
  71.2 4.5 %collective-permute-start.3 = (bf16[2,128,4096]{2,1,0:T(8,128)(2,1)S(1)}, bf16[2,128,4096]{2,1,0:T(8,128)(2,1)S(1)}, u32[]{:S(2)}, u32[]{:S(2)}) collective-permute-start(bf16[2,128,4096]{2,1,0:T(8,128)(2,1)S(1)} %bitcast.13), channel_id=1, source_target_pairs={{0,8},{8,0},{1,9},{9,1},{2,10},{10,2},{3,11},{11,3},{4,12},{12,4},... | collective-permute-start | bytes 6291464 | tf_op jit(solution)/shard_map/ppermute | solution.py:249
  71.3 4.4 %collective-permute-start.4 = (bf16[3,128,256]{2,1,0:T(8,128)(2,1)S(1)}, bf16[3,128,256]{2,1,0:T(8,128)(2,1)S(1)}, u32[]{:S(2)}, u32[]{:S(2)}) collective-permute-start(bf16[3,128,256]{2,1,0:T(8,128)(2,1)S(1)} %get-tuple-element.26), channel_id=1, source_target_pairs={{0,8},{8,0},{1,9},{9,1},{2,10},{10,2},{3,11},{11,3},{4,12},{12,4},... | collective-permute-start | bytes 589832 | tf_op jit(solution)/shard_map/ppermute | solution.py:250
